TPU v7x, 32 devices: a whole 2x2x4 slice. The times are simulated.
32 devices in a mesh: fsdp: 8 (over y, x, core), tp: 4 (over z).
Axes of the slice: x: 2, y: 2, z: 4, core: 2. Of those that a mesh axis runs over, the one named last changes fastest.
Arguments:
- w_gate: float32 [3072, 8192], P('fsdp', 'tp'), may hold values from -0.15625 to 0.15625
- first_gate: float32 [3072, 8192], P('fsdp', 'tp'), may hold values from -0.109375 to 0.109375
- second_gate: float32 [3072, 8192], P('fsdp', 'tp'), may hold values from -0.109375 to 0.109375
- w_up: float32 [3072, 8192], P('fsdp', 'tp'), may hold values from -0.15625 to 0.15625
- first_up: float32 [3072, 8192], P('fsdp', 'tp'), may hold values from -0.109375 to 0.109375
- second_up: float32 [3072, 8192], P('fsdp', 'tp'), may hold values from -0.109375 to 0.109375
- norm_train: float32 [3072], P(('fsdp', 'tp')), may hold values from 0.25 to 1.75
- norm_step: float32 [3072], P(('fsdp', 'tp')), may hold values from -0.3 to 0.3
Outputs:
- serving_gate: bfloat16 [3072, 8192], P(None, 'tp')
- serving_up: bfloat16 [3072, 8192], P(None, 'tp')
- scale_gate: float32 [8192], P('tp')
- scale_up: float32 [8192], P('tp')
- serve_norm: bfloat16 [3072], replicated
- whole_gate: float32 [3072, 8192], P('fsdp', 'tp')
- whole_up: float32 [3072, 8192], P('fsdp', 'tp')
All inputs are finite; a program needn't handle non-finite values. Where the computation divides by a largest or mean magnitude, that divisor is 1e-20 or more.
Results may differ from a plain program's by a relative error of at most 0.001.
Values may be sent and summed in bfloat16 or wider, within the bound.
A program may use at most 128 MiB of HBM per device.

v0:
```python
import jax
import jax.numpy as jnp
from jax import lax
from jax.sharding import PartitionSpec as P

D_MODEL = 3072


learn_rate = 0.25
hold_rate = 0.9


def per_device(w_gate, first_gate, second_gate, w_up, first_up, second_up, norm_train, norm_step):
    hold_gate = hold_rate * first_gate + second_gate
    whole_gate = w_gate - learn_rate * hold_gate
    hold_up = hold_rate * first_up + second_up
    whole_up = w_up - learn_rate * hold_up
    total_gate, total_up = lax.psum(
        (jnp.sum(jnp.abs(whole_gate), axis=0), jnp.sum(jnp.abs(whole_up), axis=0)), "fsdp"
    )
    scale_gate = total_gate / D_MODEL
    scale_up = total_up / D_MODEL
    narrow_gate, narrow_up = (
        (whole_gate / scale_gate).astype(jnp.bfloat16),
        (whole_up / scale_up).astype(jnp.bfloat16),
    )
    serving_gate, serving_up = (
        lax.all_gather(narrow_gate, "fsdp", axis=0, tiled=True),
        lax.all_gather(narrow_up, "fsdp", axis=0, tiled=True),
    )
    serve_norm = lax.all_gather(
        (norm_train + norm_step).astype(jnp.bfloat16), ("fsdp", "tp"), axis=0, tiled=True
    )
    return (serving_gate, serving_up, scale_gate, scale_up, serve_norm, whole_gate, whole_up)


def solution(mesh):
    return jax.shard_map(
        per_device,
        mesh=mesh,
        in_specs=(
            P("fsdp", "tp"),
            P("fsdp", "tp"),
            P("fsdp", "tp"),
            P("fsdp", "tp"),
            P("fsdp", "tp"),
            P("fsdp", "tp"),
            P(("fsdp", "tp")),
            P(("fsdp", "tp")),
        ),
        out_specs=(
            P(None, "tp"),
            P(None, "tp"),
            P("tp"),
            P("tp"),
            P(),
            P("fsdp", "tp"),
            P("fsdp", "tp"),
        ),
        check_vma=False,
    )
```

profile of v0, /device:TPU:0, one launch (start us, length us, event | category | flops | bytes accessed | tf_op | source)
XLA Modules:
  0.0 216.5 jit_solution(5402808466696674405)
XLA Ops:
  7.2 0.0 all-gather.5.cloned.1.call-start
  7.2 10.7 %abs_reduce_fusion = (f32[2048]{0:T(1024)S(1)}, f32[384,2048]{1,0:T(8,128)S(1)}, f32[2048]{0:T(1024)S(1)}, f32[384,2048]{1,0:T(8,128)}) fusion(f32[384,2048]{1,0:T(8,128)} %param.11, f32[384,2048]{1,0:T(8,128)} %param.13, f32[384,2048]{1,0:T(8,128)} %param.12, f32[384,2048]{1,0:T(8,128)} %param.8, f32[384,2048]{1,0:T(8,128)} %param.10, f32[384,2048]{1,0:T(8,128)} %param.9), kind=kLoop, calls=%fused_computation.1 | loop fusion | flops 9433088 | bytes 25182208 | tf_op jit(solution)/shard_map/reduce_sum | solution.py:19
  18.0 0.0 copy-start.1
  18.0 25.5 %all-reduce.1 = (f32[2048]{0:T(1024)S(1)}, f32[2048]{0:T(1024)S(1)}) all-reduce(f32[2048]{0:T(1024)S(1)} %get-tuple-element.13, f32[2048]{0:T(1024)S(1)} %get-tuple-element.9), channel_id=1, replica_groups=mesh['fsdp'=8,'tp'=4] {'fsdp'}, use_global_device_ids=true, to_apply=%region_1.0 | all-reduce | flops 4096 | bytes 32768 | tf_op jit(solution)/shard_map/psum | solution.py:18
  43.5 1.5 divide_convert_fusion
  45.0 0.0 all-gather.5.cloned.1.call-update
  45.0 0.0 copy-done.1
  45.0 0.0 copy-done.2
  45.0 0.0 all-gather.3.cloned.1.call-start
  45.1 0.0 copy-start.3
  45.1 0.0 copy-start.4
  45.1 0.0 copy-start.5
  45.1 3.4 %divide_convert_fusion.1 = bf16[384,2048]{1,0:T(8,128)(2,1)} fusion(f32[384,2048]{1,0:T(8,128)} %get-tuple-element.27, f32[2048]{0:T(1024)S(1)} %broadcast_multiply_fusion.1), kind=kLoop, calls=%fused_computation.3 | loop fusion | flops 1572864 | bytes 4726784 | tf_op jit(solution)/shard_map/convert_element_type | solution.py:24
  48.5 0.0 all-gather.3.cloned.1.call-update
  48.5 0.0 copy-done.3
  48.5 0.0 copy-done.4
  48.5 0.0 copy-done.5
  48.6 0.2 dynamic-update-slice
  48.8 40.7 %all-reduce = bf16[3072]{0:T(1024)(128)(2,1)} all-reduce(bf16[3072]{0:T(1024)(128)(2,1)S(1)} %dynamic-update-slice), channel_id=1, replica_groups=mesh['fsdp'=8,'tp'=4] {'fsdp','tp'}, use_global_device_ids=true, to_apply=%add | all-reduce | flops 3072 | bytes 12288
  89.5 27.9 %all-gather.5.cloned.1.call-done = bf16[3072,2048]{1,0:T(8,128)(2,1)} async-done(((bf16[384,2048]{1,0:T(8,128)(2,1)}), bf16[3072,2048]{1,0:T(8,128)(2,1)}) %all-gather.5.cloned.1.call-update) | async-done | bytes 12582928 | tf_op jit(solution)/shard_map/all_gather | solution.py:29
  117.5 74.5 %all-gather.3.cloned.1.call-done = bf16[3072,2048]{1,0:T(8,128)(2,1)} async-done(((bf16[384,2048]{1,0:T(8,128)(2,1)}), bf16[3072,2048]{1,0:T(8,128)(2,1)}) %all-gather.3.cloned.1.call-update) | async-done | bytes 12582928 | tf_op jit(solution)/shard_map/all_gather | solution.py:28
  192.0 11.4 %copy.18 = bf16[3072,2048]{1,0:T(8,128)(2,1)} copy(bf16[3072,2048]{1,0:T(8,128)(2,1)} %all-gather.3.cloned.1.call-done) | data formatting | bytes 25165824
  203.3 1.5 copy-done
  204.9 4.8 %copy.19 = bf16[3072,2048]{1,0:T(8,128)(2,1)} copy(bf16[3072,2048]{1,0:T(8,128)(2,1)S(1)} %copy-done) | data formatting | bytes 25165824
  (6 shorter events, 0.0 us)
Async XLA Ops:
  7.2 110.3 %all-gather.5.cloned.1.call-start = ((), (), s32[]{:S(2)}) async-start(), calls=%async_computation.1 | async-start | bytes 14155776 | tf_op jit(solution)/shard_map/all_gather | solution.py:29
  18.0 27.0 %copy-start.1 = (f32[384,2048]{1,0:T(8,128)}, f32[384,2048]{1,0:T(8,128)S(1)}, u32[]{:S(2)}) copy-start(f32[384,2048]{1,0:T(8,128)S(1)} %get-tuple-element.28) | copy-start | bytes 9437188
  43.5 1.5 copy-start.2
  45.0 146.9 %all-gather.3.cloned.1.call-start = ((), (), s32[]{:S(2)}) async-start(), calls=%async_computation | async-start | bytes 14155776 | tf_op jit(solution)/shard_map/all_gather | solution.py:28
  45.1 3.4 %copy-start.3 = (f32[2048]{0:T(1024)}, f32[2048]{0:T(1024)S(1)}, u32[]{:S(2)}) copy-start(f32[2048]{0:T(1024)S(1)} %broadcast_multiply_fusion.1) | copy-start | bytes 24580
  45.1 3.4 %copy-start.4 = (f32[96]{0:T(128)S(1)}, f32[96]{0:T(128)}, u32[]{:S(2)}) copy-start(f32[96]{0:T(128)} %param.14) | copy-start | bytes 1156
  45.1 3.4 %copy-start.5 = (f32[96]{0:T(128)S(1)}, f32[96]{0:T(128)}, u32[]{:S(2)}) copy-start(f32[96]{0:T(128)} %param.15) | copy-start | bytes 1156
  192.0 12.9 %copy-start = (bf16[3072,2048]{1,0:T(8,128)(2,1)S(1)}, bf16[3072,2048]{1,0:T(8,128)(2,1)}, u32[]{:S(2)}) copy-start(bf16[3072,2048]{1,0:T(8,128)(2,1)} %all-gather.5.cloned.1.call-done) | copy-start | bytes 37748740
Sparse Core Ops, SparseCore 0:
  45.1 72.3 all-gather.4
  119.9 71.9 all-gather.2
where the time goes:
time: 217 us; the launch traced here: 216 us
  waiting for transfers between devices  102 us (47%)
  blocking collectives  66.2 us (31%)
  local copies, waits for them, and re-layouts  18 us (8%)
  other arithmetic  15.6 us (7%)
  between operations  14.1 us (6%)
    all_gather x1, waiting for transfers between devices, per_device(): lax.all_gather(narrow_gate, 'fsdp', axis=0, tiled=True)  74.5 us
    unnamed x1, blocking collectives  40.7 us
    all_gather x1, waiting for transfers between devices, per_device(): lax.all_gather(narrow_up, 'fsdp', axis=0, tiled=True)  27.9 us
    psum x1, blocking collectives, per_device(): lax.psum((jnp.sum(jnp.abs(whole_gate), axis=0), jnp.sum(jnp.abs(whole_up)...  25.5 us
    unnamed x16, local copies, waits for them, and re-layouts  18 us
    reduce_sum x1, other arithmetic, per_device(): jnp.sum(jnp.abs(whole_up), axis=0)  10.7 us
  transfers between devices with their start and end apart: 2, of which 2 were waited for; matrix products, arithmetic and copies ran while one was open for 2% of the time, Pallas kernels for 0%

commit v1 on v0

v1 whole, which is shorter than its diff:
```python
import functools

import jax
import jax.numpy as jnp
from jax import lax
from jax.experimental import pallas as pl
from jax.experimental.pallas import tpu as pltpu
from jax.sharding import PartitionSpec as P

LEARN_RATE = 0.25
HOLD_RATE = 0.9
WIDTH = 512
STEP_ROWS = 16


def fused(F, T, R, C, D, S, w_gate, first_gate, second_gate, w_up, first_up, second_up, norm_train, norm_step,
          serving_gate, serving_up, scales, norm_rows, whole_gate, whole_up,
          stage, stats, norm_parts, in_sems, stat_send, stat_recv, part_send, part_recv, row_send, row_recv,
          ring_send, ring_recv, sib_send, sib_recv):
    ins = ((w_gate, first_gate, second_gate), (w_up, first_up, second_up))
    serving = (serving_gate, serving_up)
    whole = (whole_gate, whole_up)
    W = min(WIDTH, C)
    K = C // W
    units = [(m, k) for m in range(2) for k in range(K)]
    U = len(units)
    n = F // 2
    h = n // 2
    Y = n // 2
    me = lax.axis_index("fsdp")
    mt = lax.axis_index("tp")
    chip, core = lax.div(me, 2), lax.rem(me, 2)
    cy, cx = lax.div(chip, 2), lax.rem(chip, 2)
    pos = (1 - cx) * cy + cx * (n - 1 - cy)

    def chip_at(p):
        p = lax.rem(p + n, n)
        flag = lax.div(p, Y)
        return (1 - flag) * (2 * p) + flag * (2 * (n - 1 - p) + 1)

    right = chip_at(pos + 1) * 2 + core
    left = chip_at(pos - 1) * 2 + core
    sib = me + 1 - 2 * core

    def load(u, j):
        m, k = units[u]
        cols = pl.ds(k * W, W)
        return pltpu.make_async_copy(ins[m][j].at[:, cols], stage.at[3 * m + j, :, cols], in_sems.at[3 * u + j])

    for u in range(U):
        for j in range(3):
            load(u, j).start()

    barrier = pltpu.get_barrier_semaphore()
    for d in range(1, F):
        pl.semaphore_signal(barrier, inc=1, device_id={"fsdp": lax.rem(me + d, F)})
    for d in range(1, T):
        pl.semaphore_signal(barrier, inc=1, device_id={"tp": lax.rem(mt + d, T)})

    def unit_stats(u):
        m, k = units[u]
        cols = pl.ds(k * W, W)
        for j in range(3):
            load(u, j).wait()

        def body(i, acc):
            rows = pl.ds(pl.multiple_of(i * STEP_ROWS, STEP_ROWS), STEP_ROWS)
            hold = HOLD_RATE * stage[3 * m + 1, rows, cols] + stage[3 * m + 2, rows, cols]
            new = stage[3 * m, rows, cols] - LEARN_RATE * hold
            whole[m][rows, cols] = new
            mag = jnp.abs(new)
            return acc + mag[:8] + mag[8:]

        acc = lax.fori_loop(0, R // STEP_ROWS, body, jnp.zeros((8, W), jnp.float32))
        stats[me, :, pl.ds(u * W, W)] = jnp.sum(acc, axis=0, keepdims=True)

    def stat_copy(g, d, owner):
        cols = pl.ds(0, W) if g == 0 else pl.ds(W, (U - 1) * W)
        ref = stats.at[owner, :, cols]
        return pltpu.make_async_remote_copy(
            src_ref=ref, dst_ref=ref, send_sem=stat_send.at[g, d], recv_sem=stat_recv.at[g, d],
            device_id={"fsdp": lax.rem(me + d, F)})

    def unit_narrow(u):
        m, k = units[u]
        cols = pl.ds(k * W, W)
        total = stats[0, :, pl.ds(u * W, W)]
        for f in range(1, F):
            total = total + stats[f, :, pl.ds(u * W, W)]
        scale = total / D
        scales[:, pl.ds(u * W, W)] = scale
        inverse = jnp.broadcast_to(1.0 / scale, (STEP_ROWS, W))

        def body(i, carry):
            rows = pl.ds(pl.multiple_of(i * STEP_ROWS, STEP_ROWS), STEP_ROWS)
            to = pl.ds(pl.multiple_of(me * R + i * STEP_ROWS, STEP_ROWS), STEP_ROWS)
            serving[m][to, cols] = (whole[m][rows, cols] * inverse).astype(jnp.bfloat16)
            return carry

        lax.fori_loop(0, R // STEP_ROWS, body, 0)

    def block(u, f, direction, s):
        m, k = units[u]
        start, size = f * R, R
        if s == h:
            size = R // 2
            start = start + direction * size
        return serving[m].at[pl.ds(pl.multiple_of(start, 16), size), pl.ds(k * W, W)]

    def origin(direction, s):
        return chip_at(pos - s) if direction == 0 else chip_at(pos + s)

    def ring_out(u, direction, s):
        ref = block(u, origin(direction, s - 1) * 2 + core, direction, s)
        return pltpu.make_async_remote_copy(
            src_ref=ref, dst_ref=ref, send_sem=ring_send.at[direction, s - 1, u],
            recv_sem=ring_recv.at[direction, s - 1, u], device_id={"fsdp": left if direction else right})

    def ring_in(u, direction, s):
        ref = block(u, origin(direction, s) * 2 + core, direction, s)
        return pltpu.make_async_remote_copy(
            src_ref=ref, dst_ref=ref, send_sem=ring_send.at[direction, s - 1, u],
            recv_sem=ring_recv.at[direction, s - 1, u], device_id={"fsdp": left if direction else right})

    def sib_copy(u, direction, s, at_core):
        if s == 0:
            ref, i = block(u, chip * 2 + at_core, 0, 0), 0
        else:
            ref, i = block(u, origin(direction, s) * 2 + at_core, direction, s), 2 * s - 1 + direction
        return pltpu.make_async_remote_copy(
            src_ref=ref, dst_ref=ref, send_sem=sib_send.at[i, u], recv_sem=sib_recv.at[i, u],
            device_id={"fsdp": sib})

    def part_copy(d, owner):
        ref = norm_parts.at[owner]
        return pltpu.make_async_remote_copy(
            src_ref=ref, dst_ref=ref, send_sem=part_send.at[d], recv_sem=part_recv.at[d],
            device_id={"tp": lax.rem(mt + d, T)})

    def row_copy(d, owner):
        ref = norm_rows.at[owner]
        return pltpu.make_async_remote_copy(
            src_ref=ref, dst_ref=ref, send_sem=row_send.at[d], recv_sem=row_recv.at[d],
            device_id={"fsdp": lax.rem(me + d, F)})

    gain = (norm_train[...] + norm_step[...]).astype(jnp.bfloat16)
    L = norm_rows.shape[-1]
    put = (lax.broadcasted_iota(jnp.int32, (S, L), 1)
           == lax.broadcasted_iota(jnp.int32, (S, L), 0) + mt * S)
    placed = jnp.dot(jnp.broadcast_to(gain, (8, S)), jnp.where(put, 1.0, 0.0).astype(jnp.bfloat16),
                     preferred_element_type=jnp.float32)
    norm_parts[mt] = placed[:1]

    unit_stats(0)
    pl.semaphore_wait(barrier, F - 1 + T - 1)
    for d in range(1, F):
        stat_copy(0, d, me).start()
    for d in range(1, T):
        part_copy(d, mt).start()
    for d in range(1, F):
        stat_copy(0, d, lax.rem(me - d + F, F)).wait_recv()

    def send_own(u):
        for direction in range(2):
            ring_out(u, direction, 1).start()
        sib_copy(u, 0, 0, core).start()

    unit_narrow(0)
    send_own(0)
    for u in range(1, U):
        unit_stats(u)
    for d in range(1, F):
        stat_copy(1, d, me).start()

    for d in range(1, T):
        part_copy(d, lax.rem(mt - d + T, T)).wait_recv()
    row = norm_parts[0]
    for t in range(1, T):
        row = row + norm_parts[t]
    norm_rows[me] = row
    for d in range(1, F):
        row_copy(d, me).start()

    def forward(u, s):
        for direction in range(2):
            ring_in(u, direction, s).wait_recv()
            if s < h:
                ring_out(u, direction, s + 1).start()
            sib_copy(u, direction, s, core).start()

    for d in range(1, F):
        stat_copy(1, d, lax.rem(me - d + F, F)).wait_recv()
    for u in range(1, U):
        unit_narrow(u)
        send_own(u)
    for s in range(1, h + 1):
        for u in range(U):
            forward(u, s)

    for d in range(1, F):
        row_copy(d, lax.rem(me - d + F, F)).wait_recv()
    for u in range(U):
        sib_copy(u, 0, 0, 1 - core).wait_recv()
        sib_copy(u, 0, 0, core).wait_send()
        for s in range(1, h + 1):
            for direction in range(2):
                ring_out(u, direction, s).wait_send()
                sib_copy(u, direction, s, 1 - core).wait_recv()
                sib_copy(u, direction, s, core).wait_send()
    for d in range(1, F):
        stat_copy(0, d, me).wait_send()
        stat_copy(1, d, me).wait_send()
        row_copy(d, me).wait_send()
    for d in range(1, T):
        part_copy(d, mt).wait_send()


def put_out(serving_gate, serving_up, scales, whole_gate, whole_up,
            to_serving_gate, to_serving_up, scale_gate, scale_up, to_whole_gate, to_whole_up, sems):
    copies = [
        pltpu.make_async_copy(source, target, sems.at[i])
        for i, (source, target) in enumerate((
            (serving_gate, to_serving_gate), (serving_up, to_serving_up),
            (whole_gate, to_whole_gate), (whole_up, to_whole_up)))
    ]
    for copy in copies:
        copy.start()
    C = scale_gate.shape[1]
    scale_gate[...] = scales[:, :C]
    scale_up[...] = scales[:, C:]
    for copy in copies:
        copy.wait()


def per_device(F, T, *args):
    R, C = args[0].shape
    S = args[6].shape[0]
    W = min(WIDTH, C)
    U = 2 * (C // W)
    h = F // 4
    L = -(-S * T // 128) * 128
    anywhere = pl.BlockSpec(memory_space=pl.ANY)
    vmem = pl.BlockSpec(memory_space=pltpu.VMEM)
    serving = pltpu.VMEM((R * F, C), jnp.bfloat16)
    whole = pltpu.VMEM((R, C), jnp.float32)
    dma = pltpu.SemaphoreType.DMA
    serving_gate, serving_up, scales, norm_rows, whole_gate, whole_up = pl.pallas_call(
        functools.partial(fused, F, T, R, C, R * F, S),
        out_shape=(serving, serving, pltpu.VMEM((1, 2 * C), jnp.float32), jax.ShapeDtypeStruct((F, 1, L), jnp.float32),
                   whole, whole),
        in_specs=[anywhere] * 6 + [vmem] * 2,
        out_specs=(vmem,) * 6,
        scratch_shapes=[
            pltpu.VMEM((6, R, C), jnp.float32),
            pltpu.VMEM((F, 1, U * W), jnp.float32),
            pltpu.VMEM((T, 1, L), jnp.float32),
            dma((3 * U,)),
            dma((2, F)), dma((2, F)),
            dma((T,)), dma((T,)),
            dma((F,)), dma((F,)),
            dma((2, h, U)), dma((2, h, U)),
            dma((2 * h + 1, U)), dma((2 * h + 1, U)),
        ],
        compiler_params=pltpu.CompilerParams(
            collective_id=0, has_side_effects=True, vmem_limit_bytes=24 * 1024 * 1024),
        name="fused_step",
    )(*args[:6], args[6].reshape(1, S), args[7].reshape(1, S))
    small = jax.ShapeDtypeStruct((1, C), jnp.float32)
    out = pl.pallas_call(
        put_out,
        out_shape=(jax.ShapeDtypeStruct((R * F, C), jnp.bfloat16),) * 2 + (small,) * 2
        + (jax.ShapeDtypeStruct((R, C), jnp.float32),) * 2,
        in_specs=[vmem] * 5,
        out_specs=(anywhere,) * 2 + (vmem,) * 2 + (anywhere,) * 2,
        scratch_shapes=[dma((4,))],
        compiler_params=pltpu.CompilerParams(vmem_limit_bytes=1024 * 1024),
        name="put_out",
    )(serving_gate, serving_up, scales, whole_gate, whole_up)
    serving_gate, serving_up, scale_gate, scale_up, whole_gate, whole_up = out
    serve_norm = norm_rows[:, 0, :S * T].reshape(-1).astype(jnp.bfloat16)
    return (serving_gate, serving_up, scale_gate.reshape(C), scale_up.reshape(C), serve_norm, whole_gate, whole_up)


def solution(mesh):
    F, T = mesh.shape["fsdp"], mesh.shape["tp"]
    return jax.shard_map(
        functools.partial(per_device, F, T),
        mesh=mesh,
        in_specs=(P("fsdp", "tp"),) * 6 + (P(("fsdp", "tp")),) * 2,
        out_specs=(P(None, "tp"), P(None, "tp"), P("tp"), P("tp"), P(), P("fsdp", "tp"), P("fsdp", "tp")),
        check_vma=False,
    )
```

time: 217 us -> 143 us (0.66)
  Pallas kernels: 0 us -> 132 us
  waiting for transfers between devices: 102 us -> 0 us
  blocking collectives: 66.2 us -> 0 us
  other arithmetic: 15.6 us -> 0.04 us
  between operations: 14.1 us -> 0.67 us
  local copies, waits for them, and re-layouts: 18 us -> 9.96 us
    pallas_call x0 -> x2, Pallas kernels: none -> 132 us  [the longest x1 121 us: per_device(): pl.pallas_call(functools.partial(fused, F, T, R, C, R * F, S), out_shape=...]
    all_gather x2 -> x0, waiting for transfers between devices: 102 us -> none  [the longest x1 74.5 us: per_device(): lax.all_gather(narrow_gate, 'fsdp', axis=0, tiled=True)]
    unnamed x1 -> x0, blocking collectives: 40.7 us -> none
    psum x1 -> x0, blocking collectives: 25.5 us -> none  [per_device(): lax.psum((jnp.sum(jnp.abs(whole_gate), axis=0), jnp.sum(jnp.abs(whole_up)...]
    reduce_sum x1 -> x0, other arithmetic: 10.7 us -> none  [per_device(): jnp.sum(jnp.abs(whole_up), axis=0)]
    unnamed x16 -> x6, local copies, waits for them, and re-layouts: 18 us -> 9.35 us
    convert_element_type x3 -> x1, other arithmetic: 4.85 us -> 0.04 us  [per_device(): serve_norm = norm_rows[:, 0, :S * T].reshape(-1).astype(jnp.bfloat16)]
  transfers between devices with their start and end apart: 2 -> 0, of which waited for: 2 -> 0; matrix products, arithmetic and copies ran while one was open for 2% -> 0% of each run, Pallas kernels for 0% -> 0%
where the time goes in v1:
time: 143 us; the launch traced here: 142 us
  Pallas kernels  132 us (92%)
  local copies, waits for them, and re-layouts  9.96 us (7%)
    pallas_call x1, Pallas kernels, per_device(): pl.pallas_call(functools.partial(fused, F, T, R, C, R * F, S), out_shape=...  121 us
    pallas_call x1, Pallas kernels, per_device(): pl.pallas_call(put_out, out_shape=(jax.ShapeDtypeStruct((R * F, C), jnp.b...  11.2 us
    unnamed x6, local copies, waits for them, and re-layouts  9.35 us

profile of v1, /device:TPU:0, one launch (start us, length us, event | category | flops | bytes accessed | tf_op | source)
XLA Modules:
  0.0 142.4 jit_solution(3835421315823321452)
XLA Ops:
  0.6 120.6 %fused_step.1 = (bf16[3072,2048]{1,0:T(8,128)(2,1)S(1)}, bf16[3072,2048]{1,0:T(8,128)(2,1)S(1)}, f32[1,4096]{1,0:T(1,128)S(1)}, f32[8,1,384]{2,1,0:T(1,128)}, f3...) custom-call(f32[384,2048]{1,0:T(8,128)} %w_gate.1, f32[384,2048]{1,0:T(8,128)} %first_gate.1, f32[384,2048]{1,0:T(8,128)} %second_gate.1, ...), custom_call_target="tpu_custom_call" | custom-call | tf_op jit(solution)/shard_map/fused_step/pallas_call | solution.py:247
  121.2 0.0 copy-start
  121.2 4.8 %copy-done = bf16[3072,2048]{1,0:T(8,128)(2,1)} copy-done((bf16[3072,2048]{1,0:T(8,128)(2,1)}, bf16[3072,2048]{1,0:T(8,128)(2,1)S(1)}, u32[]{:S(2)}) %copy-start) | copy-done | bytes 12582936
  126.0 0.0 copy-start.1
  126.0 4.6 %copy-done.1 = bf16[3072,2048]{1,0:T(8,128)(2,1)S(1)} copy-done((bf16[3072,2048]{1,0:T(8,128)(2,1)S(1)}, bf16[3072,2048]{1,0:T(8,128)(2,1)}, u32[]{:S(2)}) %copy-start.1) | copy-done | bytes 12582936
  130.6 0.0 copy-start.2
  130.6 11.2 %put_out.1 = (bf16[3072,2048]{1,0:T(8,128)(2,1)}, bf16[3072,2048]{1,0:T(8,128)(2,1)}, f32[1,2048]{1,0:T(1,128)}, f32[1,2048]{1,0:T(1,128)}, f32[384,2048]{1,0:T(8,128)}, /*index=5*/f32[384,2048]{1,0:T(8,128)}) custom-call(bf16[3072,2048]{1,0:T(8,128)(2,1)S(1)} %copy-done.1, bf16[3072,2048]{1,0:T(8,128)(2,1)S(1)} %get-tuple-element.20.serving_up, ...), custom_call_target="tpu_custom_call" | custom-call | tf_op jit(solution)/shard_map/put_out/pallas_call | solution.py:269
  141.7 0.0 copy-done.2
  141.8 0.6 convert_element_type.7
  (1 shorter events, 0.0 us)
Async XLA Ops:
  121.2 4.8 %copy-start = (bf16[3072,2048]{1,0:T(8,128)(2,1)}, bf16[3072,2048]{1,0:T(8,128)(2,1)S(1)}, u32[]{:S(2)}) copy-start(bf16[3072,2048]{1,0:T(8,128)(2,1)S(1)} %get-tuple-element.19.serving_gate) | copy-start | bytes 37748740
  126.0 4.6 %copy-start.1 = (bf16[3072,2048]{1,0:T(8,128)(2,1)S(1)}, bf16[3072,2048]{1,0:T(8,128)(2,1)}, u32[]{:S(2)}) copy-start(bf16[3072,2048]{1,0:T(8,128)(2,1)} %copy-done) | copy-start | bytes 37748740
  130.6 11.2 %copy-start.2 = (f32[8,1,384]{2,1,0:T(1,128)S(1)}, f32[8,1,384]{2,1,0:T(1,128)}, u32[]{:S(2)}) copy-start(f32[8,1,384]{2,1,0:T(1,128)} %get-tuple-element.28) | copy-start | bytes 36868

commit v2 on v1

--- a/solution.py
+++ b/solution.py
@@ -14,11 +14,13 @@
 
 
 def fused(F, T, R, C, D, S, w_gate, first_gate, second_gate, w_up, first_up, second_up, norm_train, norm_step,
-          serving_gate, serving_up, scales, norm_rows, whole_gate, whole_up,
+          *refs):
+    pieces = 2 * (C // min(WIDTH, C))
+    serving = refs[:pieces]
+    (scales, norm_rows, whole_gate, whole_up,
           stage, stats, norm_parts, in_sems, stat_send, stat_recv, part_send, part_recv, row_send, row_recv,
-          ring_send, ring_recv, sib_send, sib_recv):
+          ring_send, ring_recv, sib_send, sib_recv) = refs[pieces:]
     ins = ((w_gate, first_gate, second_gate), (w_up, first_up, second_up))
-    serving = (serving_gate, serving_up)
     whole = (whole_gate, whole_up)
     W = min(WIDTH, C)
     K = C // W
@@ -94,18 +96,17 @@
         def body(i, carry):
             rows = pl.ds(pl.multiple_of(i * STEP_ROWS, STEP_ROWS), STEP_ROWS)
             to = pl.ds(pl.multiple_of(me * R + i * STEP_ROWS, STEP_ROWS), STEP_ROWS)
-            serving[m][to, cols] = (whole[m][rows, cols] * inverse).astype(jnp.bfloat16)
+            serving[u][to, :] = (whole[m][rows, cols] * inverse).astype(jnp.bfloat16)
             return carry
 
         lax.fori_loop(0, R // STEP_ROWS, body, 0)
 
     def block(u, f, direction, s):
-        m, k = units[u]
         start, size = f * R, R
         if s == h:
             size = R // 2
             start = start + direction * size
-        return serving[m].at[pl.ds(pl.multiple_of(start, 16), size), pl.ds(k * W, W)]
+        return serving[u].at[pl.ds(pl.multiple_of(start, 16), size)]
 
     def origin(direction, s):
         return chip_at(pos - s) if direction == 0 else chip_at(pos + s)
@@ -215,19 +216,24 @@
         part_copy(d, mt).wait_send()
 
 
-def put_out(serving_gate, serving_up, scales, whole_gate, whole_up,
-            to_serving_gate, to_serving_up, scale_gate, scale_up, to_whole_gate, to_whole_up, sems):
-    copies = [
-        pltpu.make_async_copy(source, target, sems.at[i])
-        for i, (source, target) in enumerate((
-            (serving_gate, to_serving_gate), (serving_up, to_serving_up),
-            (whole_gate, to_whole_gate), (whole_up, to_whole_up)))
-    ]
+def put_out(*refs):
+    serving = refs[:-12]
+    (scales, norm_rows, whole_gate, whole_up, to_serving_gate, to_serving_up, scale_gate, scale_up, serve_norm,
+     to_whole_gate, to_whole_up, sems) = refs[-12:]
+    W = serving[0].shape[1]
+    K = len(serving) // 2
+    pairs = [(piece, (to_serving_gate, to_serving_up)[u // K].at[:, pl.ds(u % K * W, W)])
+             for u, piece in enumerate(serving)]
+    pairs += [(whole_gate, to_whole_gate), (whole_up, to_whole_up)]
+    copies = [pltpu.make_async_copy(source, target, sems.at[i]) for i, (source, target) in enumerate(pairs)]
     for copy in copies:
         copy.start()
     C = scale_gate.shape[1]
     scale_gate[...] = scales[:, :C]
     scale_up[...] = scales[:, C:]
+    F, _, L = norm_rows.shape
+    for f in range(F):
+        serve_norm[:, pl.ds(f * L, L)] = norm_rows[f].astype(jnp.bfloat16)
     for copy in copies:
         copy.wait()
 
@@ -241,15 +247,15 @@
     L = -(-S * T // 128) * 128
     anywhere = pl.BlockSpec(memory_space=pl.ANY)
     vmem = pl.BlockSpec(memory_space=pltpu.VMEM)
-    serving = pltpu.VMEM((R * F, C), jnp.bfloat16)
+    piece = pltpu.VMEM((R * F, W), jnp.bfloat16)
     whole = pltpu.VMEM((R, C), jnp.float32)
     dma = pltpu.SemaphoreType.DMA
-    serving_gate, serving_up, scales, norm_rows, whole_gate, whole_up = pl.pallas_call(
+    held = pl.pallas_call(
         functools.partial(fused, F, T, R, C, R * F, S),
-        out_shape=(serving, serving, pltpu.VMEM((1, 2 * C), jnp.float32), jax.ShapeDtypeStruct((F, 1, L), jnp.float32),
+        out_shape=(piece,) * U + (pltpu.VMEM((1, 2 * C), jnp.float32), pltpu.VMEM((F, 1, L), jnp.float32),
                    whole, whole),
         in_specs=[anywhere] * 6 + [vmem] * 2,
-        out_specs=(vmem,) * 6,
+        out_specs=(vmem,) * (U + 4),
         scratch_shapes=[
             pltpu.VMEM((6, R, C), jnp.float32),
             pltpu.VMEM((F, 1, U * W), jnp.float32),
@@ -269,15 +275,15 @@
     out = pl.pallas_call(
         put_out,
         out_shape=(jax.ShapeDtypeStruct((R * F, C), jnp.bfloat16),) * 2 + (small,) * 2
-        + (jax.ShapeDtypeStruct((R, C), jnp.float32),) * 2,
-        in_specs=[vmem] * 5,
-        out_specs=(anywhere,) * 2 + (vmem,) * 2 + (anywhere,) * 2,
-        scratch_shapes=[dma((4,))],
+        + (jax.ShapeDtypeStruct((1, F * L), jnp.bfloat16),) + (jax.ShapeDtypeStruct((R, C), jnp.float32),) * 2,
+        in_specs=[vmem] * (U + 4),
+        out_specs=(anywhere,) * 2 + (vmem,) * 3 + (anywhere,) * 2,
+        scratch_shapes=[dma((U + 2,))],
         compiler_params=pltpu.CompilerParams(vmem_limit_bytes=1024 * 1024),
         name="put_out",
-    )(serving_gate, serving_up, scales, whole_gate, whole_up)
-    serving_gate, serving_up, scale_gate, scale_up, whole_gate, whole_up = out
-    serve_norm = norm_rows[:, 0, :S * T].reshape(-1).astype(jnp.bfloat16)
+    )(*held)
+    serving_gate, serving_up, scale_gate, scale_up, serve_norm, whole_gate, whole_up = out
+    serve_norm = serve_norm.reshape(F, L)[:, :S * T].reshape(-1)
     return (serving_gate, serving_up, scale_gate.reshape(C), scale_up.reshape(C), serve_norm, whole_gate, whole_up)
 
 

time: 143 us -> 132 us (0.923)
  local copies, waits for them, and re-layouts: 9.96 us -> 0 us
    unnamed x6 -> x0, local copies, waits for them, and re-layouts: 9.35 us -> none
where the time goes in v2:
time: 132 us
  Pallas kernels  131 us (99%)
    pallas_call x1, Pallas kernels, per_device(): pl.pallas_call(functools.partial(fused, F, T, R, C, R * F, S), out_shape=...  120 us
    pallas_call x1, Pallas kernels, per_device(): pl.pallas_call(put_out, out_shape=(jax.ShapeDtypeStruct((R * F, C), jnp.b...  11.1 us

profile of v2, /device:TPU:0, one launch (start us, length us, event | category | flops | bytes accessed | tf_op | source)
XLA Modules:
  0.0 132.3 jit_solution(17976525976180217185)
XLA Ops:
  0.6 120.0 %fused_step.1 = (bf16[3072,512]{1,0:T(8,128)(2,1)S(1)}, bf16[3072,512]{1,0:T(8,128)(2,1)S(1)}, bf16[3072,512]{1,0:T(8,128)(2,1)S(1)}, bf16[3072,512]{1,0:T(8,128...) custom-call(f32[384,2048]{1,0:T(8,128)} %w_gate.1, ...), custom_call_target="tpu_custom_call" | custom-call | tf_op jit(solution)/shard_map/fused_step/pallas_call | solution.py:253
  120.6 11.1 %put_out.1 = (bf16[3072,2048]{1,0:T(8,128)(2,1)}, bf16[3072,2048]{1,0:T(8,128)(2,1)}, f32[1,2048]{1,0:T(1,128)}, f32[1,2048]{1,0:T(1,128)}, bf16[1,3072]{1,0:T(2...) custom-call(bf16[3072,512]{1,0:T(8,128)(2,1)S(1)} %get-tuple-element.26.refs_0_, ...), custom_call_target="tpu_custom_call" | custom-call | tf_op jit(solution)/shard_map/put_out/pallas_call | solution.py:275
  131.7 0.6 reduce

commit v3 on v2

--- a/solution.py
+++ b/solution.py
@@ -49,9 +49,8 @@
         cols = pl.ds(k * W, W)
         return pltpu.make_async_copy(ins[m][j].at[:, cols], stage.at[3 * m + j, :, cols], in_sems.at[3 * u + j])
 
-    for u in range(U):
-        for j in range(3):
-            load(u, j).start()
+    for j in range(3):
+        load(0, j).start()
 
     barrier = pltpu.get_barrier_semaphore()
     for d in range(1, F):
@@ -64,6 +63,10 @@
         cols = pl.ds(k * W, W)
         for j in range(3):
             load(u, j).wait()
+        if u == 0:
+            for later in range(1, U):
+                for j in range(3):
+                    load(later, j).start()
 
         def body(i, acc):
             rows = pl.ds(pl.multiple_of(i * STEP_ROWS, STEP_ROWS), STEP_ROWS)
@@ -101,35 +104,38 @@
 
         lax.fori_loop(0, R // STEP_ROWS, body, 0)
 
-    def block(u, f, direction, s):
+    def block(u, f, part):
         start, size = f * R, R
+        if part < 2:
+            size = R // 2
+            start = start + part * size
+        return serving[u].at[pl.ds(pl.multiple_of(start, 16), size)]
+
+    def parts(u, direction, s):
         if s == h:
-            size = R // 2
-            start = start + direction * size
-        return serving[u].at[pl.ds(pl.multiple_of(start, 16), size)]
+            return [direction]
+        return [direction, 1 - direction] if u == 0 else [2]
 
     def origin(direction, s):
         return chip_at(pos - s) if direction == 0 else chip_at(pos + s)
 
-    def ring_out(u, direction, s):
-        ref = block(u, origin(direction, s - 1) * 2 + core, direction, s)
-        return pltpu.make_async_remote_copy(
-            src_ref=ref, dst_ref=ref, send_sem=ring_send.at[direction, s - 1, u],
-            recv_sem=ring_recv.at[direction, s - 1, u], device_id={"fsdp": left if direction else right})
-
-    def ring_in(u, direction, s):
-        ref = block(u, origin(direction, s) * 2 + core, direction, s)
-        return pltpu.make_async_remote_copy(
-            src_ref=ref, dst_ref=ref, send_sem=ring_send.at[direction, s - 1, u],
-            recv_sem=ring_recv.at[direction, s - 1, u], device_id={"fsdp": left if direction else right})
-
-    def sib_copy(u, direction, s, at_core):
-        if s == 0:
-            ref, i = block(u, chip * 2 + at_core, 0, 0), 0
-        else:
-            ref, i = block(u, origin(direction, s) * 2 + at_core, direction, s), 2 * s - 1 + direction
-        return pltpu.make_async_remote_copy(
-            src_ref=ref, dst_ref=ref, send_sem=sib_send.at[i, u], recv_sem=sib_recv.at[i, u],
+    def ring_copy(u, direction, s, part, back):
+        ref = block(u, origin(direction, back) * 2 + core, part)
+        return pltpu.make_async_remote_copy(
+            src_ref=ref, dst_ref=ref, send_sem=ring_send.at[direction, s - 1, part, u],
+            recv_sem=ring_recv.at[direction, s - 1, part, u], device_id={"fsdp": left if direction else right})
+
+    def ring_out(u, direction, s, part):
+        return ring_copy(u, direction, s, part, s - 1)
+
+    def ring_in(u, direction, s, part):
+        return ring_copy(u, direction, s, part, s)
+
+    def sib_copy(u, direction, s, part, at_core):
+        ref = block(u, origin(direction, s) * 2 + at_core, part)
+        i = 0 if s == 0 else 2 * s - 1 + direction
+        return pltpu.make_async_remote_copy(
+            src_ref=ref, dst_ref=ref, send_sem=sib_send.at[i, part, u], recv_sem=sib_recv.at[i, part, u],
             device_id={"fsdp": sib})
 
     def part_copy(d, owner):
@@ -162,9 +168,10 @@
         stat_copy(0, d, lax.rem(me - d + F, F)).wait_recv()
 
     def send_own(u):
-        for direction in range(2):
-            ring_out(u, direction, 1).start()
-        sib_copy(u, 0, 0, core).start()
+        for i in range(len(parts(u, 0, 1))):
+            for direction in range(2):
+                ring_out(u, direction, 1, parts(u, direction, 1)[i]).start()
+        sib_copy(u, 0, 0, 2, core).start()
 
     unit_narrow(0)
     send_own(0)
@@ -182,12 +189,19 @@
     for d in range(1, F):
         row_copy(d, me).start()
 
-    def forward(u, s):
+    def forward(u, s, i):
         for direction in range(2):
-            ring_in(u, direction, s).wait_recv()
-            if s < h:
-                ring_out(u, direction, s + 1).start()
-            sib_copy(u, direction, s, core).start()
+            part = parts(u, direction, s)[i]
+            ring_in(u, direction, s, part).wait_recv()
+            if s + 1 < h:
+                ring_out(u, direction, s + 1, part).start()
+            elif s < h and part in (2, direction):
+                ring_out(u, direction, h, direction).start()
+            sib_copy(u, direction, s, part, core).start()
+
+    early = [(0, 1, 0)] if h > 1 else []
+    for which in early:
+        forward(*which)
 
     for d in range(1, F):
         stat_copy(1, d, lax.rem(me - d + F, F)).wait_recv()
@@ -196,18 +210,21 @@
         send_own(u)
     for s in range(1, h + 1):
         for u in range(U):
-            forward(u, s)
+            for i in range(len(parts(u, 0, s))):
+                if (u, s, i) not in early:
+                    forward(u, s, i)
 
     for d in range(1, F):
         row_copy(d, lax.rem(me - d + F, F)).wait_recv()
     for u in range(U):
-        sib_copy(u, 0, 0, 1 - core).wait_recv()
-        sib_copy(u, 0, 0, core).wait_send()
+        sib_copy(u, 0, 0, 2, 1 - core).wait_recv()
+        sib_copy(u, 0, 0, 2, core).wait_send()
         for s in range(1, h + 1):
             for direction in range(2):
-                ring_out(u, direction, s).wait_send()
-                sib_copy(u, direction, s, 1 - core).wait_recv()
-                sib_copy(u, direction, s, core).wait_send()
+                for part in parts(u, direction, s):
+                    ring_out(u, direction, s, part).wait_send()
+                    sib_copy(u, direction, s, part, 1 - core).wait_recv()
+                    sib_copy(u, direction, s, part, core).wait_send()
     for d in range(1, F):
         stat_copy(0, d, me).wait_send()
         stat_copy(1, d, me).wait_send()
@@ -233,7 +250,7 @@
     scale_up[...] = scales[:, C:]
     F, _, L = norm_rows.shape
     for f in range(F):
-        serve_norm[:, pl.ds(f * L, L)] = norm_rows[f].astype(jnp.bfloat16)
+        serve_norm[pl.ds(f * L, L)] = norm_rows[f, 0].astype(jnp.bfloat16)
     for copy in copies:
         copy.wait()
 
@@ -264,8 +281,8 @@
             dma((2, F)), dma((2, F)),
             dma((T,)), dma((T,)),
             dma((F,)), dma((F,)),
-            dma((2, h, U)), dma((2, h, U)),
-            dma((2 * h + 1, U)), dma((2 * h + 1, U)),
+            dma((2, h, 3, U)), dma((2, h, 3, U)),
+            dma((2 * h + 1, 3, U)), dma((2 * h + 1, 3, U)),
         ],
         compiler_params=pltpu.CompilerParams(
             collective_id=0, has_side_effects=True, vmem_limit_bytes=24 * 1024 * 1024),
@@ -275,7 +292,7 @@
     out = pl.pallas_call(
         put_out,
         out_shape=(jax.ShapeDtypeStruct((R * F, C), jnp.bfloat16),) * 2 + (small,) * 2
-        + (jax.ShapeDtypeStruct((1, F * L), jnp.bfloat16),) + (jax.ShapeDtypeStruct((R, C), jnp.float32),) * 2,
+        + (jax.ShapeDtypeStruct((F * L,), jnp.bfloat16),) + (jax.ShapeDtypeStruct((R, C), jnp.float32),) * 2,
         in_specs=[vmem] * (U + 4),
         out_specs=(anywhere,) * 2 + (vmem,) * 3 + (anywhere,) * 2,
         scratch_shapes=[dma((U + 2,))],
@@ -283,7 +300,8 @@
         name="put_out",
     )(*held)
     serving_gate, serving_up, scale_gate, scale_up, serve_norm, whole_gate, whole_up = out
-    serve_norm = serve_norm.reshape(F, L)[:, :S * T].reshape(-1)
+    if L > S * T:
+        serve_norm = serve_norm.reshape(F, L)[:, :S * T].reshape(-1)
     return (serving_gate, serving_up, scale_gate.reshape(C), scale_up.reshape(C), serve_norm, whole_gate, whole_up)
 
 

time: 132 us -> 132 us (level)
  no operation moved by 1% of the time
where the time goes in v3:
time: 132 us
  Pallas kernels  131 us (99%)
    pallas_call x1, Pallas kernels, per_device(): pl.pallas_call(functools.partial(fused, F, T, R, C, R * F, S), out_shape=...  120 us
    pallas_call x1, Pallas kernels, per_device(): pl.pallas_call(put_out, out_shape=(jax.ShapeDtypeStruct((R * F, C), jnp.b...  11.1 us

profile of v3, /device:TPU:0, one launch (start us, length us, event | category | flops | bytes accessed | tf_op | source)
XLA Modules:
  0.0 131.7 jit_solution(13644891766363302963)
XLA Ops:
  0.6 120.0 %fused_step.1 = (bf16[3072,512]{1,0:T(8,128)(2,1)S(1)}, bf16[3072,512]{1,0:T(8,128)(2,1)S(1)}, bf16[3072,512]{1,0:T(8,128)(2,1)S(1)}, bf16[3072,512]{1,0:T(8,128...) custom-call(f32[384,2048]{1,0:T(8,128)} %w_gate.1, ...), custom_call_target="tpu_custom_call" | custom-call | tf_op jit(solution)/shard_map/fused_step/pallas_call | solution.py:270
  120.7 11.1 %put_out.1 = (bf16[3072,2048]{1,0:T(8,128)(2,1)}, bf16[3072,2048]{1,0:T(8,128)(2,1)}, f32[1,2048]{1,0:T(1,128)}, f32[1,2048]{1,0:T(1,128)}, bf16[3072]{0:T(1024)...) custom-call(bf16[3072,512]{1,0:T(8,128)(2,1)S(1)} %get-tuple-element.26.refs_0_, ...), custom_call_target="tpu_custom_call" | custom-call | tf_op jit(solution)/shard_map/put_out/pallas_call | solution.py:292

commit v4 on v3

--- a/solution.py
+++ b/solution.py
@@ -9,23 +9,26 @@
 
 LEARN_RATE = 0.25
 HOLD_RATE = 0.9
-WIDTH = 512
 STEP_ROWS = 16
+
+
+def units_of(C):
+    q = C // 4
+    return [(0, 0, q), (0, q, q), (0, 2 * q, 2 * q), (1, 0, 2 * q), (1, 2 * q, q), (1, 3 * q, q)]
 
 
 def fused(F, T, R, C, D, S, w_gate, first_gate, second_gate, w_up, first_up, second_up, norm_train, norm_step,
           *refs):
-    pieces = 2 * (C // min(WIDTH, C))
+    pieces = len(units_of(C))
     serving = refs[:pieces]
     (scales, norm_rows, whole_gate, whole_up,
           stage, stats, norm_parts, in_sems, stat_send, stat_recv, part_send, part_recv, row_send, row_recv,
           ring_send, ring_recv, sib_send, sib_recv) = refs[pieces:]
     ins = ((w_gate, first_gate, second_gate), (w_up, first_up, second_up))
     whole = (whole_gate, whole_up)
-    W = min(WIDTH, C)
-    K = C // W
-    units = [(m, k) for m in range(2) for k in range(K)]
+    units = units_of(C)
     U = len(units)
+    first = units[0][2]
     n = F // 2
     h = n // 2
     Y = n // 2
@@ -45,8 +48,8 @@
     sib = me + 1 - 2 * core
 
     def load(u, j):
-        m, k = units[u]
-        cols = pl.ds(k * W, W)
+        m, k, W = units[u]
+        cols = pl.ds(k, W)
         return pltpu.make_async_copy(ins[m][j].at[:, cols], stage.at[3 * m + j, :, cols], in_sems.at[3 * u + j])
 
     for j in range(3):
@@ -59,8 +62,8 @@
         pl.semaphore_signal(barrier, inc=1, device_id={"tp": lax.rem(mt + d, T)})
 
     def unit_stats(u):
-        m, k = units[u]
-        cols = pl.ds(k * W, W)
+        m, k, W = units[u]
+        cols = pl.ds(k, W)
         for j in range(3):
             load(u, j).wait()
         if u == 0:
@@ -77,23 +80,23 @@
             return acc + mag[:8] + mag[8:]
 
         acc = lax.fori_loop(0, R // STEP_ROWS, body, jnp.zeros((8, W), jnp.float32))
-        stats[me, :, pl.ds(u * W, W)] = jnp.sum(acc, axis=0, keepdims=True)
+        stats[me, :, pl.ds(m * C + k, W)] = jnp.sum(acc, axis=0, keepdims=True)
 
     def stat_copy(g, d, owner):
-        cols = pl.ds(0, W) if g == 0 else pl.ds(W, (U - 1) * W)
+        cols = pl.ds(0, first) if g == 0 else pl.ds(first, 2 * C - first)
         ref = stats.at[owner, :, cols]
         return pltpu.make_async_remote_copy(
             src_ref=ref, dst_ref=ref, send_sem=stat_send.at[g, d], recv_sem=stat_recv.at[g, d],
             device_id={"fsdp": lax.rem(me + d, F)})
 
     def unit_narrow(u):
-        m, k = units[u]
-        cols = pl.ds(k * W, W)
-        total = stats[0, :, pl.ds(u * W, W)]
+        m, k, W = units[u]
+        cols = pl.ds(k, W)
+        total = stats[0, :, pl.ds(m * C + k, W)]
         for f in range(1, F):
-            total = total + stats[f, :, pl.ds(u * W, W)]
+            total = total + stats[f, :, pl.ds(m * C + k, W)]
         scale = total / D
-        scales[:, pl.ds(u * W, W)] = scale
+        scales[:, pl.ds(m * C + k, W)] = scale
         inverse = jnp.broadcast_to(1.0 / scale, (STEP_ROWS, W))
 
         def body(i, carry):
@@ -237,10 +240,8 @@
     serving = refs[:-12]
     (scales, norm_rows, whole_gate, whole_up, to_serving_gate, to_serving_up, scale_gate, scale_up, serve_norm,
      to_whole_gate, to_whole_up, sems) = refs[-12:]
-    W = serving[0].shape[1]
-    K = len(serving) // 2
-    pairs = [(piece, (to_serving_gate, to_serving_up)[u // K].at[:, pl.ds(u % K * W, W)])
-             for u, piece in enumerate(serving)]
+    pairs = [(piece, (to_serving_gate, to_serving_up)[m].at[:, pl.ds(k, W)])
+             for piece, (m, k, W) in zip(serving, units_of(to_serving_gate.shape[1]))]
     pairs += [(whole_gate, to_whole_gate), (whole_up, to_whole_up)]
     copies = [pltpu.make_async_copy(source, target, sems.at[i]) for i, (source, target) in enumerate(pairs)]
     for copy in copies:
@@ -258,24 +259,24 @@
 def per_device(F, T, *args):
     R, C = args[0].shape
     S = args[6].shape[0]
-    W = min(WIDTH, C)
-    U = 2 * (C // W)
+    units = units_of(C)
+    U = len(units)
     h = F // 4
     L = -(-S * T // 128) * 128
     anywhere = pl.BlockSpec(memory_space=pl.ANY)
     vmem = pl.BlockSpec(memory_space=pltpu.VMEM)
-    piece = pltpu.VMEM((R * F, W), jnp.bfloat16)
+    pieces = tuple(pltpu.VMEM((R * F, W), jnp.bfloat16) for _, _, W in units)
     whole = pltpu.VMEM((R, C), jnp.float32)
     dma = pltpu.SemaphoreType.DMA
     held = pl.pallas_call(
         functools.partial(fused, F, T, R, C, R * F, S),
-        out_shape=(piece,) * U + (pltpu.VMEM((1, 2 * C), jnp.float32), pltpu.VMEM((F, 1, L), jnp.float32),
+        out_shape=pieces + (pltpu.VMEM((1, 2 * C), jnp.float32), pltpu.VMEM((F, 1, L), jnp.float32),
                    whole, whole),
         in_specs=[anywhere] * 6 + [vmem] * 2,
         out_specs=(vmem,) * (U + 4),
         scratch_shapes=[
             pltpu.VMEM((6, R, C), jnp.float32),
-            pltpu.VMEM((F, 1, U * W), jnp.float32),
+            pltpu.VMEM((F, 1, 2 * C), jnp.float32),
             pltpu.VMEM((T, 1, L), jnp.float32),
             dma((3 * U,)),
             dma((2, F)), dma((2, F)),

time: 132 us -> 131 us (level)
  no operation moved by 1% of the time
where the time goes in v4:
time: 131 us
  Pallas kernels  130 us (99%)
    pallas_call x1, Pallas kernels, per_device(): pl.pallas_call(functools.partial(fused, F, T, R, C, R * F, S), out_shape=...  119 us
    pallas_call x1, Pallas kernels, per_device(): pl.pallas_call(put_out, out_shape=(jax.ShapeDtypeStruct((R * F, C), jnp.b...  11 us

profile of v4, /device:TPU:0, one launch (start us, length us, event | category | flops | bytes accessed | tf_op | source)
XLA Modules:
  0.0 130.7 jit_solution(8416378825711779001)
XLA Ops:
  0.6 119.0 %fused_step.1 = (bf16[3072,512]{1,0:T(8,128)(2,1)S(1)}, bf16[3072,512]{1,0:T(8,128)(2,1)S(1)}, bf16[3072,1024]{1,0:T(8,128)(2,1)S(1)}, bf16[3072,1024]{1,0:T(8,1...) custom-call(f32[384,2048]{1,0:T(8,128)} %w_gate.1, ...), custom_call_target="tpu_custom_call" | custom-call | tf_op jit(solution)/shard_map/fused_step/pallas_call | solution.py:271
  119.6 11.0 %put_out.1 = (bf16[3072,2048]{1,0:T(8,128)(2,1)}, bf16[3072,2048]{1,0:T(8,128)(2,1)}, f32[1,2048]{1,0:T(1,128)}, f32[1,2048]{1,0:T(1,128)}, bf16[3072]{0:T(1024)...) custom-call(bf16[3072,512]{1,0:T(8,128)(2,1)S(1)} %get-tuple-element.24.refs_0_, ...), custom_call_target="tpu_custom_call" | custom-call | tf_op jit(solution)/shard_map/put_out/pallas_call | solution.py:293
